TPU v7x, 32 devices: a whole 2x2x4 slice. The times are simulated.
32 devices in a mesh: inp: 8 (over z, y), tm: 4 (over x, core).
Axes of the slice: x: 2, y: 2, z: 4, core: 2. Of those that a mesh axis runs over, the one named last changes fastest.
Arguments:
- voltages: bfloat16 [1024, 262144], P('inp', 'tm'), may hold values from -6 to 6
- pfb_coeff: float32 [16, 512], replicated, may hold values from -1.5 to 1.5
Outputs:
- visibilities: float32 [32, 2, 1024, 1024], P(('inp', 'tm'))
All inputs are finite; a program needn't handle non-finite values.
Results may differ from a plain program's by a relative error of at most 0.0029.
Values may be sent and summed in bfloat16 or wider, within the bound.
A program may use at most 128 MiB of HBM per device.

v0:
```python
import functools
import math

import jax
import jax.numpy as jnp
import numpy as np
from jax import lax
from jax.experimental import pallas as pl
from jax.experimental.pallas import tpu as pltpu
from jax.sharding import PartitionSpec as P

LANES = 128
ROWS = 16
GROUP = 8
CHUNK = 16
NT = (((1,), (1,)), ((), ()))


def dft_tables(channels, length):
    phase = np.arange(channels)[:, None] * np.arange(length)[None, :] % length
    angle = phase * (2.0 * math.pi / length)
    table = np.stack([np.cos(angle), -np.sin(angle)], axis=1) / math.sqrt(length)
    table = table.reshape(2 * channels, length).astype(np.float32)
    high = table.astype(jnp.bfloat16)
    low = (table - high.astype(np.float32)).astype(jnp.bfloat16)
    return np.concatenate([high, low], axis=0)


def channelize_kernel(
    n_inp, n_tm, volt, coef_in, table, out,
    slab, coef, high0, low0, high1, low1, stage, send,
    load_sem, tail_send, tail_recv, send_sem, recv_sem,
):
    in_rows = volt.shape[0]
    taps, length = coef_in.shape
    spec = volt.shape[1] // length
    lines = stage.shape[0] // CHUNK
    n_dev = n_inp * n_tm
    chunks = spec // CHUNK
    tail = (taps - 1) * length
    width = CHUNK * length
    a_tiles = in_rows // ROWS
    inp = lax.axis_index("inp")
    tm = lax.axis_index("tm")
    me = inp * n_tm + tm

    def load(q):
        return pltpu.make_async_copy(
            volt.at[:, pl.ds(pl.multiple_of(q * width, width), width)],
            slab.at[:, pl.ds(pl.multiple_of(tail + q * width, length), width)],
            load_sem.at[q],
        )

    load(0).start()
    load(1).start()

    barrier = pltpu.get_barrier_semaphore()

    def greet(d, _):
        other = lax.rem(me + d, n_dev)
        pl.semaphore_signal(
            barrier, inc=1, device_id=(other // n_tm, lax.rem(other, n_tm)),
            device_id_type=pl.DeviceIdType.MESH,
        )
        return _

    lax.fori_loop(1, n_dev, greet, 0)
    for j in range(taps):
        coef[j] = jnp.broadcast_to(coef_in[j : j + 1, :], (8, length))
    @pl.when(tm == 0)
    def _():
        def clear(e, _):
            slab[:, pl.ds(pl.multiple_of(e * length, length), length)] = jnp.zeros(
                (in_rows, length), slab.dtype
            )
            return _

        lax.fori_loop(0, taps - 1, clear, 0)

    f_high, f_low = (high0, high1), (low0, low1)

    def fir(first, tile, slot):
        row = pl.multiple_of(tile * ROWS, ROWS)
        for nt in range(length // LANES):
            lanes = pl.ds(nt * LANES, LANES)
            c = [coef[j, :, lanes] for j in range(taps)]
            low = [None] * GROUP
            high = [None] * GROUP
            for t in range(GROUP + taps - 1):
                col = pl.multiple_of((first + t) * length + nt * LANES, LANES)
                x = slab[pl.ds(row, ROWS), pl.ds(col, LANES)].astype(jnp.float32)
                x0, x1 = x[:8], x[8:]
                for i in range(max(0, t - taps + 1), min(GROUP - 1, t) + 1):
                    w = c[t - i]
                    if t == i:
                        low[i], high[i] = w * x0, w * x1
                    else:
                        low[i], high[i] = low[i] + w * x0, high[i] + w * x1
                i = t - taps + 1
                if i >= 0:
                    f = jnp.concatenate([low[i], high[i]], axis=0)
                    h = f.astype(jnp.bfloat16)
                    f_high[slot][i, pl.ds(row, ROWS), lanes] = h
                    f_low[slot][i, pl.ds(row, ROWS), lanes] = (
                        f - h.astype(jnp.float32)
                    ).astype(jnp.bfloat16)

    def dft(tile, slot):
        per = GROUP // a_tiles
        for u in range(per):
            i = tile * per + u
            r = lax.dot_general(table[...], f_high[slot][i], NT, preferred_element_type=jnp.float32)
            r2 = lax.dot_general(table[:lines], f_low[slot][i], NT, preferred_element_type=jnp.float32)
            stage[pl.ds(slot * GROUP + i, lines, stride=CHUNK), :] = r[:lines] + r[lines:] + r2

    def each(body):
        def step(tile, _):
            body(tile)
            return _

        lax.fori_loop(0, a_tiles, step, 0)

    def own(q):
        return pltpu.make_async_copy(send.at[q, me], place(out, q), recv_sem)

    def place(ref, q):
        first = pl.multiple_of(tm * spec + q * CHUNK, CHUNK)
        return ref.at[inp, :, pl.ds(first, CHUNK), :]

    def dispatch(q):
        def convert(d, _):
            rows = pl.ds(pl.multiple_of(d * 2 * CHUNK, 2 * CHUNK), 2 * CHUNK)
            send[q, d] = stage[rows, :].reshape(2, CHUNK, in_rows).astype(send.dtype)
            return _

        lax.fori_loop(0, n_dev, convert, 0)

        def post(d, _):
            other = lax.rem(me + d, n_dev)
            pltpu.make_async_remote_copy(
                src_ref=send.at[q, other], dst_ref=place(out, q),
                send_sem=send_sem, recv_sem=recv_sem,
                device_id=(other // n_tm, lax.rem(other, n_tm)),
                device_id_type=pl.DeviceIdType.MESH,
            ).start()
            return _

        lax.fori_loop(1, n_dev, post, 0)
        own(q).start()

    def chunk_of(k):
        return lax.rem(k + 1, chunks)

    load(0).wait()
    load(1).wait()
    for q in range(2, chunks):
        load(q).start()
    each(lambda tile: fir(chunk_of(0) * CHUNK, tile, 0))
    pl.semaphore_wait(barrier, n_dev - 1)

    history = pltpu.make_async_remote_copy(
        src_ref=volt.at[:, pl.ds(spec * length - tail, tail)],
        dst_ref=slab.at[:, pl.ds(0, tail)],
        send_sem=tail_send, recv_sem=tail_recv,
        device_id=(inp, lax.rem(tm + 1, n_tm)),
        device_id_type=pl.DeviceIdType.MESH,
    )

    @pl.when(tm < n_tm - 1)
    def _():
        history.start()

    def turn(k, carry):
        q = chunk_of(k)
        later = chunk_of(k + 1)

        def second(tile):
            dft(tile, 0)
            fir(q * CHUNK + GROUP, tile, 1)

        each(second)

        @pl.when(later > 0)
        def _():
            load(later).wait()

        @pl.when((later == 0) & (tm > 0))
        def _():
            history.wait_recv()

        def first(tile):
            dft(tile, 1)
            fir(later * CHUNK, tile, 0)

        each(first)
        dispatch(q)
        return carry

    lax.fori_loop(0, chunks - 1, turn, 0)

    def final(tile):
        dft(tile, 0)
        fir(GROUP, tile, 1)

    each(final)
    each(lambda tile: dft(tile, 1))
    dispatch(0)

    @pl.when(tm < n_tm - 1)
    def _():
        history.wait_send()

    sent = send.at[:, pl.ds(0, n_dev - 1)]
    pltpu.make_async_copy(sent, sent, send_sem).wait()
    pltpu.make_async_copy(out, out, recv_sem).wait()


def correlate_kernel(z_ref, o_ref, wide, turned, crossed):
    groups, _, spectra, in_rows = z_ref.shape
    block = o_ref.shape[2]

    @pl.when(pl.program_id(0) == 0)
    def _():
        for g in range(groups):
            cols = slice(g * in_rows, (g + 1) * in_rows)
            for p in range(2):
                part = z_ref[g, p]
                wide[p * spectra : (p + 1) * spectra, cols] = part
                flip = part.T
                turned[cols, p * spectra : (p + 1) * spectra] = flip
                crossed[cols, (1 - p) * spectra : (2 - p) * spectra] = flip if p else -flip

    rows = pl.ds(pl.multiple_of(pl.program_id(0) * block, block), block)
    scale = 1.0 / spectra
    o_ref[0, 0] = jnp.dot(turned[rows, :], wide[...], preferred_element_type=jnp.float32) * scale
    o_ref[0, 1] = jnp.dot(crossed[rows, :], wide[...], preferred_element_type=jnp.float32) * scale


def per_device(voltages, pfb_coeff):
    n_inp = lax.axis_size("inp")
    n_tm = lax.axis_size("tm")
    channels = n_inp * n_tm
    in_rows = voltages.shape[0]
    taps, length = pfb_coeff.shape
    spec = voltages.shape[1] // length
    lines = 2 * channels
    table = jnp.asarray(dft_tables(channels, length))
    vmem = pl.BlockSpec(memory_space=pltpu.VMEM)
    hbm = pl.BlockSpec(memory_space=pl.ANY)
    bf16 = jnp.bfloat16
    received = pl.pallas_call(
        functools.partial(channelize_kernel, n_inp, n_tm),
        out_shape=jax.ShapeDtypeStruct((n_inp, 2, n_tm * spec, in_rows), bf16),
        in_specs=[hbm, vmem, vmem],
        out_specs=hbm,
        scratch_shapes=[
            pltpu.VMEM((in_rows, (spec + taps - 1) * length), bf16),
            pltpu.VMEM((taps, 8, length), jnp.float32),
            pltpu.VMEM((GROUP, in_rows, length), bf16),
            pltpu.VMEM((GROUP, in_rows, length), bf16),
            pltpu.VMEM((GROUP, in_rows, length), bf16),
            pltpu.VMEM((GROUP, in_rows, length), bf16),
            pltpu.VMEM((lines * CHUNK, in_rows), jnp.float32),
            pltpu.VMEM((spec // CHUNK, channels, 2, CHUNK, in_rows), bf16),
            pltpu.SemaphoreType.DMA((spec // CHUNK,)),
            pltpu.SemaphoreType.DMA,
            pltpu.SemaphoreType.DMA,
            pltpu.SemaphoreType.DMA,
            pltpu.SemaphoreType.DMA,
        ],
        compiler_params=pltpu.CompilerParams(
            collective_id=0, has_side_effects=True, vmem_limit_bytes=60 * 1024 * 1024
        ),
        name="channelize",
    )(voltages, pfb_coeff, table)
    inputs = n_inp * in_rows
    spectra = n_tm * spec
    block = min(256, inputs)
    return pl.pallas_call(
        correlate_kernel,
        grid=(inputs // block,),
        out_shape=jax.ShapeDtypeStruct((1, 2, inputs, inputs), jnp.float32),
        in_specs=[pl.BlockSpec(received.shape, lambda i: (0, 0, 0, 0))],
        out_specs=pl.BlockSpec((1, 2, block, inputs), lambda i: (0, 0, i, 0)),
        scratch_shapes=[
            pltpu.VMEM((2 * spectra, inputs), bf16),
            pltpu.VMEM((inputs, 2 * spectra), bf16),
            pltpu.VMEM((inputs, 2 * spectra), bf16),
        ],
        compiler_params=pltpu.CompilerParams(vmem_limit_bytes=60 * 1024 * 1024),
        name="correlate",
    )(received)


def solution(mesh):
    return jax.shard_map(
        per_device,
        mesh=mesh,
        in_specs=(P("inp", "tm"), P()),
        out_specs=P(("inp", "tm"), None, None, None),
        check_vma=False,
    )
```

profile of v0, /device:TPU:0, one launch (start us, length us, event | category | flops | bytes accessed | tf_op | source)
XLA Modules:
  0.0 81.3 jit_solution(5065372954715691785)
XLA Ops:
  0.0 72.3 %channelize.1.z_ref = bf16[8,2,512,128]{3,2,1,0:T(8,128)(2,1)} custom-call(bf16[128,65536]{1,0:T(8,128)(2,1)} %volt.1, f32[16,512]{1,0:T(8,128)} %coef_in.1, bf16[128,512]{1,0:T(8,128)(2,1)} %constant.2.clone.table), custom_call_target="tpu_custom_call" | custom-call | tf_op jit(solution)/shard_map/channelize/pallas_call | solution.py:251
  72.3 9.0 %correlate.1 = f32[1,2,1024,1024]{3,2,1,0:T(8,128)} custom-call(bf16[8,2,512,128]{3,2,1,0:T(8,128)(2,1)} %channelize.1.z_ref), custom_call_target="tpu_custom_call" | custom-call | tf_op jit(solution)/shard_map/correlate/pallas_call | solution.py:279
where the time goes:
time: 81.5 us; the launch traced here: 81.3 us
  Pallas kernels  81.3 us (100%)
    pallas_call x1, Pallas kernels, per_device(): pl.pallas_call(functools.partial(channelize_kernel, n_inp, n_tm), out_sha...  72.3 us
    pallas_call x1, Pallas kernels, per_device(): pl.pallas_call(correlate_kernel, grid=(inputs // block,), out_shape=jax.S...  9.01 us

commit v1 on v0

--- a/solution.py
+++ b/solution.py
@@ -236,7 +236,7 @@
     o_ref[0, 1] = jnp.dot(crossed[rows, :], wide[...], preferred_element_type=jnp.float32) * scale
 
 
-def per_device(voltages, pfb_coeff):
+def narrow_device(voltages, pfb_coeff):
     n_inp = lax.axis_size("inp")
     n_tm = lax.axis_size("tm")
     channels = n_inp * n_tm
@@ -292,6 +292,272 @@
     )(received)
 
 
+STEP = 8
+PART = 4
+
+
+def split_table(channels, length):
+    phase = np.arange(channels)[:, None] * np.arange(length)[None, :] % length
+    angle = phase * (2.0 * math.pi / length)
+    table = np.stack([np.cos(angle), -np.sin(angle)], axis=1) / math.sqrt(length)
+    return table.reshape(2 * channels, length).astype(np.float32)
+
+
+def stream_kernel(
+    n_inp, n_tm, volt, coef_in, table, out,
+    slab, taps_table, prod, acc, head, tail_out, tail_in, stage, send,
+    load_sem, tail_send, tail_recv, send_sem, recv_sem,
+):
+    in_rows = volt.shape[0]
+    taps, length = coef_in.shape
+    steps = volt.shape[1] // (length * STEP)
+    lines = table.shape[0]
+    n_dev = n_inp * n_tm
+    width = STEP * length
+    inp = lax.axis_index("inp")
+    tm = lax.axis_index("tm")
+    me = inp * n_tm + tm
+    heads = (taps + STEP - 1) // STEP
+    turn = steps - heads
+
+    def load(i):
+        cols = pl.ds(pl.multiple_of(i * width, width), width)
+        return pltpu.make_async_copy(volt.at[:, cols], slab.at[:, cols], load_sem.at[i])
+
+    def step_of(t):
+        return lax.rem(t + heads, steps)
+
+    for t in range(steps):
+        load((t + heads) % steps).start()
+
+    barrier = pltpu.get_barrier_semaphore()
+
+    def greet(d, _):
+        other = lax.rem(me + d, n_dev)
+        pl.semaphore_signal(
+            barrier, inc=1, device_id=(other // n_tm, lax.rem(other, n_tm)),
+            device_id_type=pl.DeviceIdType.MESH,
+        )
+        return _
+
+    lax.fori_loop(1, n_dev, greet, 0)
+
+    def build(j, _):
+        full = table[...] * coef_in[pl.ds(j, 1), :]
+        high = full.astype(jnp.bfloat16)
+        rows = pl.ds(pl.multiple_of(j * lines, lines), lines)
+        taps_table[rows, :length] = high
+        taps_table[rows, length:] = (full - high.astype(jnp.float32)).astype(jnp.bfloat16)
+        return _
+
+    lax.fori_loop(0, taps, build, 0)
+    acc[...] = jnp.zeros(acc.shape, acc.dtype)
+
+    half = n_inp // 2
+    side = inp // half
+    fars = [(1 - side) * half + lax.rem(inp + d, half) for d in range(half)]
+    nears = [side * half + lax.rem(inp + d, half) for d in range(half)]
+    cores = [lax.rem(tm + d, n_tm) for d in range(n_tm)]
+
+    def place(i):
+        return out.at[inp, tm * steps + i]
+
+    def dispatch(i):
+        send[i] = stage[...].reshape(n_dev, 2 * STEP, in_rows).astype(send.dtype)
+
+        def post(inp2, tm2):
+            pltpu.make_async_remote_copy(
+                src_ref=send.at[i, inp2 * n_tm + tm2], dst_ref=place(i),
+                send_sem=send_sem, recv_sem=recv_sem,
+                device_id=(inp2, tm2), device_id_type=pl.DeviceIdType.MESH,
+            ).start()
+
+        for row in fars:
+            for core in cores:
+                post(row, core)
+        for d, row in enumerate(nears):
+            for core in cores[d == 0 :]:
+                post(row, core)
+        pltpu.make_async_copy(send.at[i, me], place(i), recv_sem).start()
+
+    def advance(i):
+        first = i * width
+        for h in range(STEP // PART):
+            x = jnp.concatenate(
+                [
+                    slab[:, pl.ds(pl.multiple_of(first + (h * PART + u) * length, length), length)]
+                    for u in range(PART)
+                ],
+                axis=0,
+            )
+            x = jnp.concatenate([x, x], axis=1)
+            prod[h] = lax.dot_general(taps_table[...], x, NT, preferred_element_type=jnp.float32)
+            for k in range(taps + PART - 1):
+                total = acc[k] if k < taps - 1 else None
+                for u in range(PART):
+                    j = u + taps - 1 - k
+                    if 0 <= j < taps:
+                        term = prod[h, j * lines : (j + 1) * lines, u * in_rows : (u + 1) * in_rows]
+                        total = term if total is None else total + term
+                if k < PART:
+                    stage[pl.ds(h * PART + k, lines, stride=STEP), :] = total
+                else:
+                    acc[k - PART] = total
+
+    def finish(w, source):
+        for q in range(heads):
+            for k in range(STEP):
+                rows = pl.ds(k, lines, stride=STEP)
+                total = head[q + (0 if w else heads), rows, :]
+                s = q * STEP + k
+                stage[rows, :] = total + source[s] if s < taps - 1 else total
+            dispatch(q + (0 if w else heads))
+
+    history = pltpu.make_async_remote_copy(
+        src_ref=tail_out, dst_ref=tail_in, send_sem=tail_send, recv_sem=tail_recv,
+        device_id=(inp, lax.rem(tm + 1, n_tm)), device_id_type=pl.DeviceIdType.MESH,
+    )
+
+    def work(t, carry):
+        i = step_of(t)
+        load(i).wait()
+
+        @pl.when(t == heads)
+        def _():
+            pl.semaphore_wait(barrier, n_dev - 1)
+
+        @pl.when(t == turn)
+        def _():
+            tail_out[...] = acc[...]
+            acc[...] = jnp.zeros(acc.shape, acc.dtype)
+
+            @pl.when(tm < n_tm - 1)
+            def _():
+                history.start()
+
+        advance(i)
+        @pl.when((t < heads) | (t >= turn))
+        def _():
+            head[i] = stage[...]
+
+        @pl.when((t >= heads) & (t < turn))
+        def _():
+            dispatch(i)
+
+        return carry
+
+    lax.fori_loop(0, steps, work, 0)
+    finish(0, acc)
+
+    @pl.when(tm > 0)
+    def _():
+        history.wait_recv()
+
+    @pl.when(tm == 0)
+    def _():
+        tail_in[...] = jnp.zeros(tail_in.shape, tail_in.dtype)
+
+    finish(1, tail_in)
+
+    @pl.when(tm < n_tm - 1)
+    def _():
+        history.wait_send()
+
+    sent = send.at[:, pl.ds(0, n_dev - 1)]
+    pltpu.make_async_copy(sent, sent, send_sem).wait()
+    pltpu.make_async_copy(out, out, recv_sem).wait()
+
+
+def gram_kernel(z_ref, o_ref, wide, cross, turned):
+    groups, chunks, pair, in_rows = z_ref.shape
+    depth = chunks * pair
+    spectra = depth // 2
+    block = o_ref.shape[2]
+
+    @pl.when(pl.program_id(0) == 0)
+    def _():
+        for g in range(groups):
+            cols = slice(g * in_rows, (g + 1) * in_rows)
+            part = z_ref[g]
+            flat = part.reshape(depth, in_rows)
+            wide[:, cols] = flat
+            turned[cols, :] = flat.T
+            full = part.astype(jnp.float32)
+            swap = jnp.concatenate([-full[:, pair // 2 :], full[:, : pair // 2]], axis=1)
+            cross[:, cols] = swap.astype(part.dtype).reshape(depth, in_rows)
+
+    rows = pl.ds(pl.multiple_of(pl.program_id(0) * block, block), block)
+    scale = 1.0 / spectra
+    left = turned[rows, :]
+    o_ref[0, 0] = jnp.dot(left, wide[...], preferred_element_type=jnp.float32) * scale
+    o_ref[0, 1] = jnp.dot(left, cross[...], preferred_element_type=jnp.float32) * scale
+
+
+def stream_device(voltages, pfb_coeff):
+    n_inp = lax.axis_size("inp")
+    n_tm = lax.axis_size("tm")
+    channels = n_inp * n_tm
+    in_rows = voltages.shape[0]
+    taps, length = pfb_coeff.shape
+    steps = voltages.shape[1] // (length * STEP)
+    lines = 2 * channels
+    heads = (taps + STEP - 1) // STEP
+    table = jnp.asarray(split_table(channels, length))
+    vmem = pl.BlockSpec(memory_space=pltpu.VMEM)
+    hbm = pl.BlockSpec(memory_space=pl.ANY)
+    bf16, f32 = jnp.bfloat16, jnp.float32
+    carry = (taps - 1, lines, in_rows)
+    received = pl.pallas_call(
+        functools.partial(stream_kernel, n_inp, n_tm),
+        out_shape=jax.ShapeDtypeStruct((n_inp, n_tm * steps, 2 * STEP, in_rows), bf16),
+        in_specs=[hbm, vmem, vmem],
+        out_specs=hbm,
+        scratch_shapes=[
+            pltpu.VMEM(voltages.shape, bf16),
+            pltpu.VMEM((taps * lines, 2 * length), bf16),
+            pltpu.VMEM((STEP // PART, taps * lines, PART * in_rows), f32),
+            pltpu.VMEM(carry, f32),
+            pltpu.VMEM((2 * heads, lines * STEP, in_rows), f32),
+            pltpu.VMEM(carry, f32),
+            pltpu.VMEM(carry, f32),
+            pltpu.VMEM((lines * STEP, in_rows), f32),
+            pltpu.VMEM((steps, channels, 2 * STEP, in_rows), bf16),
+            pltpu.SemaphoreType.DMA((steps,)),
+            pltpu.SemaphoreType.DMA,
+            pltpu.SemaphoreType.DMA,
+            pltpu.SemaphoreType.DMA,
+            pltpu.SemaphoreType.DMA,
+        ],
+        compiler_params=pltpu.CompilerParams(
+            collective_id=0, has_side_effects=True, vmem_limit_bytes=60 * 1024 * 1024
+        ),
+        name="stream",
+    )(voltages, pfb_coeff, table)
+    inputs = n_inp * in_rows
+    depth = n_tm * steps * 2 * STEP
+    block = min(256, inputs)
+    return pl.pallas_call(
+        gram_kernel,
+        grid=(inputs // block,),
+        out_shape=jax.ShapeDtypeStruct((1, 2, inputs, inputs), f32),
+        in_specs=[pl.BlockSpec(received.shape, lambda i: (0, 0, 0, 0))],
+        out_specs=pl.BlockSpec((1, 2, block, inputs), lambda i: (0, 0, i, 0)),
+        scratch_shapes=[
+            pltpu.VMEM((depth, inputs), bf16),
+            pltpu.VMEM((depth, inputs), bf16),
+            pltpu.VMEM((inputs, depth), bf16),
+        ],
+        compiler_params=pltpu.CompilerParams(vmem_limit_bytes=60 * 1024 * 1024),
+        name="gram",
+    )(received)
+
+
+def per_device(voltages, pfb_coeff):
+    if voltages.shape[0] % LANES == 0:
+        return stream_device(voltages, pfb_coeff)
+    return narrow_device(voltages, pfb_coeff)
+
+
 def solution(mesh):
     return jax.shard_map(
         per_device,

time: 81.5 us -> 71 us (0.87)
  Pallas kernels: 81.3 us -> 70.8 us
    pallas_call x2, Pallas kernels: 81.3 us -> 70.8 us  [the longest x1 61.3 us: stream_device(): pl.pallas_call(functools.partial(stream_kernel, n_inp, n_tm), out_shape=j...]
where the time goes in v1:
time: 71 us; the launch traced here: 70.8 us
  Pallas kernels  70.8 us (100%)
    pallas_call x1, Pallas kernels, stream_device(): pl.pallas_call(functools.partial(stream_kernel, n_inp, n_tm), out_shape=j...  61.3 us
    pallas_call x1, Pallas kernels, stream_device(): pl.pallas_call(gram_kernel, grid=(inputs // block,), out_shape=jax.ShapeD...  9.47 us

profile of v1, /device:TPU:0, one launch (start us, length us, event | category | flops | bytes accessed | tf_op | source)
XLA Modules:
  0.0 70.8 jit_solution(15407751254352834850)
XLA Ops:
  0.0 61.3 %stream.1.z_ref = bf16[8,64,16,128]{3,2,1,0:T(8,128)(2,1)} custom-call(bf16[128,65536]{1,0:T(8,128)(2,1)} %volt.1, f32[16,512]{1,0:T(8,128)} %coef_in.1, f32[64,512]{1,0:T(8,128)} %constant.2.clone.table), custom_call_target="tpu_custom_call" | custom-call | tf_op jit(solution)/shard_map/stream/pallas_call | solution.py:510
  61.4 9.5 %gram.1 = f32[1,2,1024,1024]{3,2,1,0:T(8,128)} custom-call(bf16[8,64,16,128]{3,2,1,0:T(8,128)(2,1)} %stream.1.z_ref), custom_call_target="tpu_custom_call" | custom-call | tf_op jit(solution)/shard_map/gram/pallas_call | solution.py:539

commit v2 on v1

--- a/solution.py
+++ b/solution.py
@@ -294,6 +294,12 @@
 
 STEP = 8
 PART = 4
+SPAN = 4
+BLOCK = 256
+AHEAD = 3
+TINY = jnp.float8_e5m2
+LIFT = 2.0**12
+GAIN = 2.0**38
 
 
 def split_table(channels, length):
@@ -304,14 +310,14 @@
 
 
 def stream_kernel(
-    n_inp, n_tm, volt, coef_in, table, out,
-    slab, taps_table, prod, acc, head, tail_out, tail_in, stage, send,
-    load_sem, tail_send, tail_recv, send_sem, recv_sem,
+    n_inp, n_tm, volt, coef_from, table_from, part, last,
+    coef_in, table, slab, taps_table, low_table, thin, acc, head, tail_out, tail_in, stage, send,
+    landed, wide, cross, turned, small_sem, load_sem, tail_send, tail_recv, send_sem, recv_sem,
 ):
     in_rows = volt.shape[0]
-    taps, length = coef_in.shape
+    taps, length = coef_from.shape
     steps = volt.shape[1] // (length * STEP)
-    lines = table.shape[0]
+    lines = table_from.shape[0]
     n_dev = n_inp * n_tm
     width = STEP * length
     inp = lax.axis_index("inp")
@@ -327,7 +333,13 @@
     def step_of(t):
         return lax.rem(t + heads, steps)
 
-    for t in range(steps):
+    small = [
+        pltpu.make_async_copy(source, target, small_sem.at[n])
+        for n, (source, target) in enumerate(((coef_from, coef_in), (table_from, table)))
+    ]
+    for copy in small:
+        copy.start()
+    for t in range(AHEAD):
         load((t + heads) % steps).start()
 
     barrier = pltpu.get_barrier_semaphore()
@@ -341,13 +353,15 @@
         return _
 
     lax.fori_loop(1, n_dev, greet, 0)
+    for copy in small:
+        copy.wait()
 
     def build(j, _):
-        full = table[...] * coef_in[pl.ds(j, 1), :]
+        full = table[...] * coef_in[pl.ds(j, 1), :] * GAIN
         high = full.astype(jnp.bfloat16)
         rows = pl.ds(pl.multiple_of(j * lines, lines), lines)
-        taps_table[rows, :length] = high
-        taps_table[rows, length:] = (full - high.astype(jnp.float32)).astype(jnp.bfloat16)
+        taps_table[rows, :] = high
+        low_table[rows, :] = ((full - high.astype(jnp.float32)) / LIFT).astype(TINY)
         return _
 
     lax.fori_loop(0, taps, build, 0)
@@ -359,16 +373,21 @@
     nears = [side * half + lax.rem(inp + d, half) for d in range(half)]
     cores = [lax.rem(tm + d, n_tm) for d in range(n_tm)]
 
-    def place(i):
-        return out.at[inp, tm * steps + i]
+    def slot(i):
+        return me * SPAN + lax.rem(i, SPAN)
+
+    def bank(group):
+        return last if isinstance(group, int) and group == 0 else landed.at[group - 1]
 
     def dispatch(i):
-        send[i] = stage[...].reshape(n_dev, 2 * STEP, in_rows).astype(send.dtype)
+        send[i] = (stage[...] * (1.0 / GAIN)).reshape(n_dev, 2 * STEP, in_rows).astype(send.dtype)
+        group = i // SPAN
+        target = bank(group)
 
         def post(inp2, tm2):
             pltpu.make_async_remote_copy(
-                src_ref=send.at[i, inp2 * n_tm + tm2], dst_ref=place(i),
-                send_sem=send_sem, recv_sem=recv_sem,
+                src_ref=send.at[i, inp2 * n_tm + tm2], dst_ref=target.at[slot(i)],
+                send_sem=send_sem, recv_sem=recv_sem.at[group],
                 device_id=(inp2, tm2), device_id_type=pl.DeviceIdType.MESH,
             ).start()
 
@@ -378,7 +397,7 @@
         for d, row in enumerate(nears):
             for core in cores[d == 0 :]:
                 post(row, core)
-        pltpu.make_async_copy(send.at[i, me], place(i), recv_sem).start()
+        target[slot(i)] = send[i, me]
 
     def advance(i):
         first = i * width
@@ -390,14 +409,16 @@
                 ],
                 axis=0,
             )
-            x = jnp.concatenate([x, x], axis=1)
-            prod[h] = lax.dot_general(taps_table[...], x, NT, preferred_element_type=jnp.float32)
+            thin[h] = (x.astype(jnp.float32) * LIFT).astype(TINY)
+            high = lax.dot_general(taps_table[...], x, NT, preferred_element_type=jnp.float32)
+            low = lax.dot_general(low_table[...], thin[h], NT, preferred_element_type=jnp.float32)
             for k in range(taps + PART - 1):
                 total = acc[k] if k < taps - 1 else None
                 for u in range(PART):
                     j = u + taps - 1 - k
                     if 0 <= j < taps:
-                        term = prod[h, j * lines : (j + 1) * lines, u * in_rows : (u + 1) * in_rows]
+                        spot = (slice(j * lines, (j + 1) * lines), slice(u * in_rows, (u + 1) * in_rows))
+                        term = high[spot] + low[spot]
                         total = term if total is None else total + term
                 if k < PART:
                     stage[pl.ds(h * PART + k, lines, stride=STEP), :] = total
@@ -422,6 +443,10 @@
         i = step_of(t)
         load(i).wait()
 
+        @pl.when(t < steps - AHEAD)
+        def _():
+            load(step_of(t + AHEAD)).start()
+
         @pl.when(t == heads)
         def _():
             pl.semaphore_wait(barrier, n_dev - 1)
@@ -449,6 +474,27 @@
     lax.fori_loop(0, steps, work, 0)
     finish(0, acc)
 
+    def arrive(group):
+        came = bank(group).at[pl.ds(0, (n_dev - 1) * SPAN)]
+        pltpu.make_async_copy(came, came, recv_sem.at[group]).wait()
+
+    def fold(group):
+        arrive(group)
+        pack(bank(group), wide, cross, turned)
+
+        def block(b, carry):
+            rows = pl.ds(pl.multiple_of(b * BLOCK, BLOCK), BLOCK)
+            left = turned[rows, :]
+            for p, right in enumerate((wide, cross)):
+                term = jnp.dot(left, right[...], preferred_element_type=jnp.float32)
+                part[p, rows, :] = term if group == 1 else part[p, rows, :] + term
+            return carry
+
+        lax.fori_loop(0, part.shape[1] // BLOCK, block, 0)
+
+    for group in range(1, steps // SPAN - 1):
+        fold(group)
+
     @pl.when(tm > 0)
     def _():
         history.wait_recv()
@@ -458,6 +504,7 @@
         tail_in[...] = jnp.zeros(tail_in.shape, tail_in.dtype)
 
     finish(1, tail_in)
+    fold(steps // SPAN - 1)
 
     @pl.when(tm < n_tm - 1)
     def _():
@@ -465,32 +512,39 @@
 
     sent = send.at[:, pl.ds(0, n_dev - 1)]
     pltpu.make_async_copy(sent, sent, send_sem).wait()
-    pltpu.make_async_copy(out, out, recv_sem).wait()
-
-
-def gram_kernel(z_ref, o_ref, wide, cross, turned):
-    groups, chunks, pair, in_rows = z_ref.shape
-    depth = chunks * pair
-    spectra = depth // 2
-    block = o_ref.shape[2]
-
-    @pl.when(pl.program_id(0) == 0)
-    def _():
-        for g in range(groups):
-            cols = slice(g * in_rows, (g + 1) * in_rows)
-            part = z_ref[g]
-            flat = part.reshape(depth, in_rows)
-            wide[:, cols] = flat
-            turned[cols, :] = flat.T
-            full = part.astype(jnp.float32)
-            swap = jnp.concatenate([-full[:, pair // 2 :], full[:, : pair // 2]], axis=1)
-            cross[:, cols] = swap.astype(part.dtype).reshape(depth, in_rows)
-
-    rows = pl.ds(pl.multiple_of(pl.program_id(0) * block, block), block)
+    arrive(0)
+
+
+def pack(source, wide, cross, turned):
+    depth, inputs = wide.shape
+    tiles, pair, in_rows = source.shape
+    span = depth // pair
+    for g in range(inputs // in_rows):
+        cols = slice(g * in_rows, (g + 1) * in_rows)
+        piece = source[g * span : (g + 1) * span]
+        flat = piece.reshape(depth, in_rows)
+        wide[:, cols] = flat
+        turned[cols, :] = flat.T
+        full = piece.astype(jnp.float32)
+        swap = jnp.concatenate([-full[:, pair // 2 :], full[:, : pair // 2]], axis=1)
+        cross[:, cols] = swap.astype(piece.dtype).reshape(depth, in_rows)
+
+
+def close_kernel(spectra, part, last, out, wide, cross, turned, done, sem):
+    pack(last, wide, cross, turned)
     scale = 1.0 / spectra
-    left = turned[rows, :]
-    o_ref[0, 0] = jnp.dot(left, wide[...], preferred_element_type=jnp.float32) * scale
-    o_ref[0, 1] = jnp.dot(left, cross[...], preferred_element_type=jnp.float32) * scale
+    copies = []
+    for b in range(part.shape[1] // BLOCK):
+        rows = slice(b * BLOCK, (b + 1) * BLOCK)
+        left = turned[rows, :]
+        for p, right in enumerate((wide, cross)):
+            term = jnp.dot(left, right[...], preferred_element_type=jnp.float32)
+            done[p, rows, :] = (part[p, rows, :] + term) * scale
+            copies.append(
+                pltpu.make_async_copy(done.at[p, rows, :], out.at[0, p, rows, :], sem)
+            )
+            copies[-1].start()
+    pltpu.make_async_copy(done, out.at[0], sem).wait()
 
 
 def stream_device(voltages, pfb_coeff):
@@ -507,49 +561,56 @@
     hbm = pl.BlockSpec(memory_space=pl.ANY)
     bf16, f32 = jnp.bfloat16, jnp.float32
     carry = (taps - 1, lines, in_rows)
-    received = pl.pallas_call(
+    inputs = n_inp * in_rows
+    depth = n_tm * SPAN * 2 * STEP
+    tiles = (channels * SPAN, 2 * STEP, in_rows)
+    gram = (2, inputs, inputs)
+    operands = [
+        pltpu.VMEM((depth, inputs), bf16),
+        pltpu.VMEM((depth, inputs), bf16),
+        pltpu.VMEM((inputs, depth), bf16),
+    ]
+    part, last = pl.pallas_call(
         functools.partial(stream_kernel, n_inp, n_tm),
-        out_shape=jax.ShapeDtypeStruct((n_inp, n_tm * steps, 2 * STEP, in_rows), bf16),
-        in_specs=[hbm, vmem, vmem],
-        out_specs=hbm,
+        out_shape=[pltpu.VMEM(gram, f32), pltpu.VMEM(tiles, bf16)],
+        in_specs=[hbm, hbm, hbm],
+        out_specs=[vmem, vmem],
         scratch_shapes=[
+            pltpu.VMEM(pfb_coeff.shape, f32),
+            pltpu.VMEM(table.shape, f32),
             pltpu.VMEM(voltages.shape, bf16),
-            pltpu.VMEM((taps * lines, 2 * length), bf16),
-            pltpu.VMEM((STEP // PART, taps * lines, PART * in_rows), f32),
+            pltpu.VMEM((taps * lines, length), bf16),
+            pltpu.VMEM((taps * lines, length), TINY),
+            pltpu.VMEM((STEP // PART, PART * in_rows, length), TINY),
             pltpu.VMEM(carry, f32),
             pltpu.VMEM((2 * heads, lines * STEP, in_rows), f32),
             pltpu.VMEM(carry, f32),
             pltpu.VMEM(carry, f32),
             pltpu.VMEM((lines * STEP, in_rows), f32),
             pltpu.VMEM((steps, channels, 2 * STEP, in_rows), bf16),
+            pltpu.VMEM((steps // SPAN - 1, *tiles), bf16),
+            *operands,
+            pltpu.SemaphoreType.DMA((2,)),
             pltpu.SemaphoreType.DMA((steps,)),
             pltpu.SemaphoreType.DMA,
             pltpu.SemaphoreType.DMA,
             pltpu.SemaphoreType.DMA,
-            pltpu.SemaphoreType.DMA,
+            pltpu.SemaphoreType.DMA((steps // SPAN,)),
         ],
         compiler_params=pltpu.CompilerParams(
-            collective_id=0, has_side_effects=True, vmem_limit_bytes=60 * 1024 * 1024
+            collective_id=0, has_side_effects=True, vmem_limit_bytes=44 * 1024 * 1024
         ),
         name="stream",
-    )(voltages, pfb_coeff, table)
-    inputs = n_inp * in_rows
-    depth = n_tm * steps * 2 * STEP
-    block = min(256, inputs)
+    )(*(pltpu.with_memory_space_constraint(x, pltpu.HBM) for x in (voltages, pfb_coeff, table)))
     return pl.pallas_call(
-        gram_kernel,
-        grid=(inputs // block,),
-        out_shape=jax.ShapeDtypeStruct((1, 2, inputs, inputs), f32),
-        in_specs=[pl.BlockSpec(received.shape, lambda i: (0, 0, 0, 0))],
-        out_specs=pl.BlockSpec((1, 2, block, inputs), lambda i: (0, 0, i, 0)),
-        scratch_shapes=[
-            pltpu.VMEM((depth, inputs), bf16),
-            pltpu.VMEM((depth, inputs), bf16),
-            pltpu.VMEM((inputs, depth), bf16),
-        ],
-        compiler_params=pltpu.CompilerParams(vmem_limit_bytes=60 * 1024 * 1024),
-        name="gram",
-    )(received)
+        functools.partial(close_kernel, n_tm * steps * STEP),
+        out_shape=jax.ShapeDtypeStruct((1, *gram), f32),
+        in_specs=[vmem, vmem],
+        out_specs=hbm,
+        scratch_shapes=[*operands, pltpu.VMEM(gram, f32), pltpu.SemaphoreType.DMA],
+        compiler_params=pltpu.CompilerParams(vmem_limit_bytes=24 * 1024 * 1024),
+        name="close",
+    )(part, last)
 
 
 def per_device(voltages, pfb_coeff):

time: 71 us -> 63.9 us (0.900)
  Pallas kernels: 70.8 us -> 63.7 us
    pallas_call x2, Pallas kernels: 70.8 us -> 63.7 us  [the longest x1 60 us: stream_device(): pl.pallas_call(functools.partial(stream_kernel, n_inp, n_tm), out_shape=[...]
where the time goes in v2:
time: 63.9 us; the launch traced here: 63.7 us
  Pallas kernels  63.7 us (100%)
    pallas_call x1, Pallas kernels, stream_device(): pl.pallas_call(functools.partial(stream_kernel, n_inp, n_tm), out_shape=[...  60 us
    pallas_call x1, Pallas kernels, stream_device(): pl.pallas_call(functools.partial(close_kernel, n_tm * steps * STEP), out_...  3.74 us

profile of v2, /device:TPU:0, one launch (start us, length us, event | category | flops | bytes accessed | tf_op | source)
XLA Modules:
  0.0 63.7 jit_solution(8516239789708520869)
XLA Ops:
  0.0 60.0 %stream.1 = (f32[2,1024,1024]{2,1,0:T(8,128)S(1)}, bf16[128,16,128]{2,1,0:T(8,128)(2,1)S(1)}) custom-call(bf16[128,65536]{1,0:T(8,128)(2,1)} %volt.1, f32[16,512]{1,0:T(8,128)} %coef_from.1, f32[64,512]{1,0:T(8,128)} %constant.2.clone.table_from), custom_call_target="tpu_custom_call" | custom-call | tf_op jit(solution)/shard_map/stream/pallas_call | solution.py:573
  60.0 3.7 %close.1 = f32[1,2,1024,1024]{3,2,1,0:T(8,128)} custom-call(f32[2,1024,1024]{2,1,0:T(8,128)S(1)} %get-tuple-element.7.part, bf16[128,16,128]{2,1,0:T(8,128)(2,1)S(1)} %get-tuple-element.8.last), custom_call_target="tpu_custom_call" | custom-call | tf_op jit(solution)/shard_map/close/pallas_call | solution.py:605

commit v3 on v2

--- a/solution.py
+++ b/solution.py
@@ -310,9 +310,9 @@
 
 
 def stream_kernel(
-    n_inp, n_tm, volt, coef_from, table_from, part, last,
+    n_inp, n_tm, volt, coef_from, table_from, part, landed,
     coef_in, table, slab, taps_table, low_table, thin, acc, head, tail_out, tail_in, stage, send,
-    landed, wide, cross, turned, small_sem, load_sem, tail_send, tail_recv, send_sem, recv_sem,
+    wide, cross, turned, small_sem, load_sem, tail_send, tail_recv, send_sem, recv_sem,
 ):
     in_rows = volt.shape[0]
     taps, length = coef_from.shape
@@ -330,9 +330,6 @@
         cols = pl.ds(pl.multiple_of(i * width, width), width)
         return pltpu.make_async_copy(volt.at[:, cols], slab.at[:, cols], load_sem.at[i])
 
-    def step_of(t):
-        return lax.rem(t + heads, steps)
-
     small = [
         pltpu.make_async_copy(source, target, small_sem.at[n])
         for n, (source, target) in enumerate(((coef_from, coef_in), (table_from, table)))
@@ -373,20 +370,14 @@
     nears = [side * half + lax.rem(inp + d, half) for d in range(half)]
     cores = [lax.rem(tm + d, n_tm) for d in range(n_tm)]
 
-    def slot(i):
-        return me * SPAN + lax.rem(i, SPAN)
-
-    def bank(group):
-        return last if isinstance(group, int) and group == 0 else landed.at[group - 1]
-
     def dispatch(i):
         send[i] = (stage[...] * (1.0 / GAIN)).reshape(n_dev, 2 * STEP, in_rows).astype(send.dtype)
         group = i // SPAN
-        target = bank(group)
+        target = landed.at[group, me * SPAN + lax.rem(i, SPAN)]
 
         def post(inp2, tm2):
             pltpu.make_async_remote_copy(
-                src_ref=send.at[i, inp2 * n_tm + tm2], dst_ref=target.at[slot(i)],
+                src_ref=send.at[i, inp2 * n_tm + tm2], dst_ref=target,
                 send_sem=send_sem, recv_sem=recv_sem.at[group],
                 device_id=(inp2, tm2), device_id_type=pl.DeviceIdType.MESH,
             ).start()
@@ -397,11 +388,13 @@
         for d, row in enumerate(nears):
             for core in cores[d == 0 :]:
                 post(row, core)
-        target[slot(i)] = send[i, me]
-
-    def advance(i):
+        target[...] = send[i, me]
+
+    def advance(i, skip=0):
         first = i * width
         for h in range(STEP // PART):
+            start = max(skip - h * PART, 0)
+            used = min(PART + taps - 1 - start, taps) * lines
             x = jnp.concatenate(
                 [
                     slab[:, pl.ds(pl.multiple_of(first + (h * PART + u) * length, length), length)]
@@ -410,9 +403,9 @@
                 axis=0,
             )
             thin[h] = (x.astype(jnp.float32) * LIFT).astype(TINY)
-            high = lax.dot_general(taps_table[...], x, NT, preferred_element_type=jnp.float32)
-            low = lax.dot_general(low_table[...], thin[h], NT, preferred_element_type=jnp.float32)
-            for k in range(taps + PART - 1):
+            high = lax.dot_general(taps_table[:used, :], x, NT, preferred_element_type=jnp.float32)
+            low = lax.dot_general(low_table[:used, :], thin[h], NT, preferred_element_type=jnp.float32)
+            for k in range(start, taps + PART - 1):
                 total = acc[k] if k < taps - 1 else None
                 for u in range(PART):
                     j = u + taps - 1 - k
@@ -425,31 +418,35 @@
                 else:
                     acc[k - PART] = total
 
-    def finish(w, source):
-        for q in range(heads):
-            for k in range(STEP):
-                rows = pl.ds(k, lines, stride=STEP)
-                total = head[q + (0 if w else heads), rows, :]
-                s = q * STEP + k
-                stage[rows, :] = total + source[s] if s < taps - 1 else total
-            dispatch(q + (0 if w else heads))
+    def finish(q):
+        for k in range(STEP):
+            rows = pl.ds(k, lines, stride=STEP)
+            total = head[q, rows, :]
+            s = q * STEP + k
+            stage[rows, :] = total + tail_in[s] if s < taps - 1 else total
+        dispatch(q)
 
     history = pltpu.make_async_remote_copy(
         src_ref=tail_out, dst_ref=tail_in, send_sem=tail_send, recv_sem=tail_recv,
         device_id=(inp, lax.rem(tm + 1, n_tm)), device_id_type=pl.DeviceIdType.MESH,
     )
 
+    for t in range(heads):
+        load(t + heads).wait()
+        load(t + heads + AHEAD).start()
+        advance(t + heads, (heads - t) * STEP)
+    pl.semaphore_wait(barrier, n_dev - 1)
+
     def work(t, carry):
-        i = step_of(t)
-        load(i).wait()
+        i = lax.rem(t + heads, steps)
+
+        @pl.when(t < steps)
+        def _():
+            load(i).wait()
 
         @pl.when(t < steps - AHEAD)
         def _():
-            load(step_of(t + AHEAD)).start()
-
-        @pl.when(t == heads)
-        def _():
-            pl.semaphore_wait(barrier, n_dev - 1)
+            load(lax.rem(i + AHEAD, steps)).start()
 
         @pl.when(t == turn)
         def _():
@@ -461,26 +458,26 @@
                 history.start()
 
         advance(i)
-        @pl.when((t < heads) | (t >= turn))
+
+        @pl.when(i < heads)
         def _():
             head[i] = stage[...]
 
-        @pl.when((t >= heads) & (t < turn))
+        @pl.when(i >= heads)
         def _():
             dispatch(i)
 
         return carry
 
-    lax.fori_loop(0, steps, work, 0)
-    finish(0, acc)
+    lax.fori_loop(heads, steps + heads, work, 0)
 
     def arrive(group):
-        came = bank(group).at[pl.ds(0, (n_dev - 1) * SPAN)]
+        came = landed.at[group, pl.ds(0, (n_dev - 1) * SPAN)]
         pltpu.make_async_copy(came, came, recv_sem.at[group]).wait()
 
     def fold(group):
         arrive(group)
-        pack(bank(group), wide, cross, turned)
+        pack(landed.at[group], wide, cross, turned)
 
         def block(b, carry):
             rows = pl.ds(pl.multiple_of(b * BLOCK, BLOCK), BLOCK)
@@ -503,7 +500,8 @@
     def _():
         tail_in[...] = jnp.zeros(tail_in.shape, tail_in.dtype)
 
-    finish(1, tail_in)
+    for q in range(heads):
+        finish(q)
     fold(steps // SPAN - 1)
 
     @pl.when(tm < n_tm - 1)
@@ -530,8 +528,8 @@
         cross[:, cols] = swap.astype(piece.dtype).reshape(depth, in_rows)
 
 
-def close_kernel(spectra, part, last, out, wide, cross, turned, done, sem):
-    pack(last, wide, cross, turned)
+def close_kernel(spectra, part, landed, out, wide, cross, turned, done, sem):
+    pack(landed.at[0], wide, cross, turned)
     scale = 1.0 / spectra
     copies = []
     for b in range(part.shape[1] // BLOCK):
@@ -563,14 +561,14 @@
     carry = (taps - 1, lines, in_rows)
     inputs = n_inp * in_rows
     depth = n_tm * SPAN * 2 * STEP
-    tiles = (channels * SPAN, 2 * STEP, in_rows)
+    tiles = (steps // SPAN, channels * SPAN, 2 * STEP, in_rows)
     gram = (2, inputs, inputs)
     operands = [
         pltpu.VMEM((depth, inputs), bf16),
         pltpu.VMEM((depth, inputs), bf16),
         pltpu.VMEM((inputs, depth), bf16),
     ]
-    part, last = pl.pallas_call(
+    part, landed = pl.pallas_call(
         functools.partial(stream_kernel, n_inp, n_tm),
         out_shape=[pltpu.VMEM(gram, f32), pltpu.VMEM(tiles, bf16)],
         in_specs=[hbm, hbm, hbm],
@@ -583,12 +581,11 @@
             pltpu.VMEM((taps * lines, length), TINY),
             pltpu.VMEM((STEP // PART, PART * in_rows, length), TINY),
             pltpu.VMEM(carry, f32),
-            pltpu.VMEM((2 * heads, lines * STEP, in_rows), f32),
+            pltpu.VMEM((heads, lines * STEP, in_rows), f32),
             pltpu.VMEM(carry, f32),
             pltpu.VMEM(carry, f32),
             pltpu.VMEM((lines * STEP, in_rows), f32),
             pltpu.VMEM((steps, channels, 2 * STEP, in_rows), bf16),
-            pltpu.VMEM((steps // SPAN - 1, *tiles), bf16),
             *operands,
             pltpu.SemaphoreType.DMA((2,)),
             pltpu.SemaphoreType.DMA((steps,)),
@@ -610,7 +607,7 @@
         scratch_shapes=[*operands, pltpu.VMEM(gram, f32), pltpu.SemaphoreType.DMA],
         compiler_params=pltpu.CompilerParams(vmem_limit_bytes=24 * 1024 * 1024),
         name="close",
-    )(part, last)
+    )(part, landed)
 
 
 def per_device(voltages, pfb_coeff):

time: 63.9 us -> 62.4 us (0.977)
  Pallas kernels: 63.7 us -> 62.2 us
    pallas_call x1, Pallas kernels: 60 us -> 58.5 us  [stream_device(): pl.pallas_call(functools.partial(stream_kernel, n_inp, n_tm), out_shape=[...]
where the time goes in v3:
time: 62.4 us; the launch traced here: 62.2 us
  Pallas kernels  62.2 us (100%)
    pallas_call x1, Pallas kernels, stream_device(): pl.pallas_call(functools.partial(stream_kernel, n_inp, n_tm), out_shape=[...  58.5 us
    pallas_call x1, Pallas kernels, stream_device(): pl.pallas_call(functools.partial(close_kernel, n_tm * steps * STEP), out_...  3.73 us

profile of v3, /device:TPU:0, one launch (start us, length us, event | category | flops | bytes accessed | tf_op | source)
XLA Modules:
  0.0 62.2 jit_solution(8762156327287294220)
XLA Ops:
  0.0 58.5 %stream.1 = (f32[2,1024,1024]{2,1,0:T(8,128)S(1)}, bf16[4,128,16,128]{3,2,1,0:T(8,128)(2,1)S(1)}) custom-call(bf16[128,65536]{1,0:T(8,128)(2,1)} %volt.1, f32[16,512]{1,0:T(8,128)} %coef_from.1, f32[64,512]{1,0:T(8,128)} %constant.2.clone.table_from), custom_call_target="tpu_custom_call" | custom-call | tf_op jit(solution)/shard_map/stream/pallas_call | solution.py:571
  58.5 3.7 %close.1 = f32[1,2,1024,1024]{3,2,1,0:T(8,128)} custom-call(f32[2,1024,1024]{2,1,0:T(8,128)S(1)} %get-tuple-element.7.part, bf16[4,128,16,128]{3,2,1,0:T(8,128)(2,1)S(1)} %get-tuple-element.8.landed), custom_call_target="tpu_custom_call" | custom-call | tf_op jit(solution)/shard_map/close/pallas_call | solution.py:602

commit v4 on v3

--- a/solution.py
+++ b/solution.py
@@ -324,7 +324,8 @@
     tm = lax.axis_index("tm")
     me = inp * n_tm + tm
     heads = (taps + STEP - 1) // STEP
-    turn = steps - heads
+    origin = steps // 2
+    turn = steps - origin
 
     def load(i):
         cols = pl.ds(pl.multiple_of(i * width, width), width)
@@ -337,7 +338,7 @@
     for copy in small:
         copy.start()
     for t in range(AHEAD):
-        load((t + heads) % steps).start()
+        load((t + origin) % steps).start()
 
     barrier = pltpu.get_barrier_semaphore()
 
@@ -350,19 +351,21 @@
         return _
 
     lax.fori_loop(1, n_dev, greet, 0)
+    acc[...] = jnp.zeros(acc.shape, acc.dtype)
     for copy in small:
         copy.wait()
+
+    early = min(STEP + taps - 1 - heads * STEP, taps)
 
     def build(j, _):
         full = table[...] * coef_in[pl.ds(j, 1), :] * GAIN
         high = full.astype(jnp.bfloat16)
-        rows = pl.ds(pl.multiple_of(j * lines, lines), lines)
+        rows = pl.ds(j * lines if isinstance(j, int) else pl.multiple_of(j * lines, lines), lines)
         taps_table[rows, :] = high
         low_table[rows, :] = ((full - high.astype(jnp.float32)) / LIFT).astype(TINY)
         return _
 
-    lax.fori_loop(0, taps, build, 0)
-    acc[...] = jnp.zeros(acc.shape, acc.dtype)
+    lax.fori_loop(0, early, build, 0)
 
     half = n_inp // 2
     side = inp // half
@@ -370,10 +373,10 @@
     nears = [side * half + lax.rem(inp + d, half) for d in range(half)]
     cores = [lax.rem(tm + d, n_tm) for d in range(n_tm)]
 
-    def dispatch(i):
+    def dispatch(i, place):
         send[i] = (stage[...] * (1.0 / GAIN)).reshape(n_dev, 2 * STEP, in_rows).astype(send.dtype)
-        group = i // SPAN
-        target = landed.at[group, me * SPAN + lax.rem(i, SPAN)]
+        group = place // SPAN
+        target = landed.at[group, me * SPAN + place % SPAN]
 
         def post(inp2, tm2):
             pltpu.make_async_remote_copy(
@@ -390,10 +393,12 @@
                 post(row, core)
         target[...] = send[i, me]
 
-    def advance(i, skip=0):
+    def advance(i, skip=0, stop=STEP + taps - 1):
         first = i * width
         for h in range(STEP // PART):
             start = max(skip - h * PART, 0)
+            end = min(stop - h * PART, PART + taps - 1)
+            base = max(taps - end, 0) * lines
             used = min(PART + taps - 1 - start, taps) * lines
             x = jnp.concatenate(
                 [
@@ -403,14 +408,14 @@
                 axis=0,
             )
             thin[h] = (x.astype(jnp.float32) * LIFT).astype(TINY)
-            high = lax.dot_general(taps_table[:used, :], x, NT, preferred_element_type=jnp.float32)
-            low = lax.dot_general(low_table[:used, :], thin[h], NT, preferred_element_type=jnp.float32)
-            for k in range(start, taps + PART - 1):
+            high = lax.dot_general(taps_table[base:used, :], x, NT, preferred_element_type=jnp.float32)
+            low = lax.dot_general(low_table[base:used, :], thin[h], NT, preferred_element_type=jnp.float32)
+            for k in range(start, end):
                 total = acc[k] if k < taps - 1 else None
                 for u in range(PART):
                     j = u + taps - 1 - k
                     if 0 <= j < taps:
-                        spot = (slice(j * lines, (j + 1) * lines), slice(u * in_rows, (u + 1) * in_rows))
+                        spot = (slice(j * lines - base, (j + 1) * lines - base), slice(u * in_rows, (u + 1) * in_rows))
                         term = high[spot] + low[spot]
                         total = term if total is None else total + term
                 if k < PART:
@@ -424,7 +429,7 @@
             total = head[q, rows, :]
             s = q * STEP + k
             stage[rows, :] = total + tail_in[s] if s < taps - 1 else total
-        dispatch(q)
+        dispatch(q, steps - heads + q)
 
     history = pltpu.make_async_remote_copy(
         src_ref=tail_out, dst_ref=tail_in, send_sem=tail_send, recv_sem=tail_recv,
@@ -432,13 +437,21 @@
     )
 
     for t in range(heads):
-        load(t + heads).wait()
-        load(t + heads + AHEAD).start()
-        advance(t + heads, (heads - t) * STEP)
+        load(t + origin).wait()
+        load((t + origin + AHEAD) % steps).start()
+        advance(t + origin, (heads - t) * STEP)
+        if t == 0:
+            for j in range(early, taps):
+                build(j, None)
+    load(origin + heads).wait()
+    load((origin + heads + AHEAD) % steps).start()
     pl.semaphore_wait(barrier, n_dev - 1)
+    advance(origin + heads, 0, STEP)
+    dispatch(origin + heads, 0)
+    advance(origin + heads, STEP)
 
     def work(t, carry):
-        i = lax.rem(t + heads, steps)
+        i = lax.rem(t + origin, steps)
 
         @pl.when(t < steps)
         def _():
@@ -465,11 +478,22 @@
 
         @pl.when(i >= heads)
         def _():
-            dispatch(i)
+            dispatch(i, lax.rem(i + steps - 2 * heads - origin, steps - heads))
 
         return carry
 
-    lax.fori_loop(heads, steps + heads, work, 0)
+    lax.fori_loop(heads + 1, steps + heads, work, 0)
+
+    @pl.when(tm > 0)
+    def _():
+        history.wait_recv()
+
+    @pl.when(tm == 0)
+    def _():
+        tail_in[...] = jnp.zeros(tail_in.shape, tail_in.dtype)
+
+    for q in range(heads):
+        finish(q)
 
     def arrive(group):
         came = landed.at[group, pl.ds(0, (n_dev - 1) * SPAN)]
@@ -484,25 +508,13 @@
             left = turned[rows, :]
             for p, right in enumerate((wide, cross)):
                 term = jnp.dot(left, right[...], preferred_element_type=jnp.float32)
-                part[p, rows, :] = term if group == 1 else part[p, rows, :] + term
+                part[p, rows, :] = term if group == 0 else part[p, rows, :] + term
             return carry
 
         lax.fori_loop(0, part.shape[1] // BLOCK, block, 0)
 
-    for group in range(1, steps // SPAN - 1):
+    for group in range(steps // SPAN - 1):
         fold(group)
-
-    @pl.when(tm > 0)
-    def _():
-        history.wait_recv()
-
-    @pl.when(tm == 0)
-    def _():
-        tail_in[...] = jnp.zeros(tail_in.shape, tail_in.dtype)
-
-    for q in range(heads):
-        finish(q)
-    fold(steps // SPAN - 1)
 
     @pl.when(tm < n_tm - 1)
     def _():
@@ -510,7 +522,7 @@
 
     sent = send.at[:, pl.ds(0, n_dev - 1)]
     pltpu.make_async_copy(sent, sent, send_sem).wait()
-    arrive(0)
+    arrive(steps // SPAN - 1)
 
 
 def pack(source, wide, cross, turned):
@@ -529,7 +541,7 @@
 
 
 def close_kernel(spectra, part, landed, out, wide, cross, turned, done, sem):
-    pack(landed.at[0], wide, cross, turned)
+    pack(landed.at[landed.shape[0] - 1], wide, cross, turned)
     scale = 1.0 / spectra
     copies = []
     for b in range(part.shape[1] // BLOCK):

time: 62.4 us -> 62.4 us (level)
  no operation moved by 1% of the time
where the time goes in v4:
time: 62.4 us; the launch traced here: 62.2 us
  Pallas kernels  62.2 us (100%)
    pallas_call x1, Pallas kernels, stream_device(): pl.pallas_call(functools.partial(stream_kernel, n_inp, n_tm), out_shape=[...  58.5 us
    pallas_call x1, Pallas kernels, stream_device(): pl.pallas_call(functools.partial(close_kernel, n_tm * steps * STEP), out_...  3.74 us

profile of v4, /device:TPU:0, one launch (start us, length us, event | category | flops | bytes accessed | tf_op | source)
XLA Modules:
  0.0 62.2 jit_solution(11413667976776669878)
XLA Ops:
  0.0 58.5 %stream.1 = (f32[2,1024,1024]{2,1,0:T(8,128)S(1)}, bf16[4,128,16,128]{3,2,1,0:T(8,128)(2,1)S(1)}) custom-call(bf16[128,65536]{1,0:T(8,128)(2,1)} %volt.1, f32[16,512]{1,0:T(8,128)} %coef_from.1, f32[64,512]{1,0:T(8,128)} %constant.2.clone.table_from), custom_call_target="tpu_custom_call" | custom-call | tf_op jit(solution)/shard_map/stream/pallas_call | solution.py:583
  58.5 3.7 %close.1 = f32[1,2,1024,1024]{3,2,1,0:T(8,128)} custom-call(f32[2,1024,1024]{2,1,0:T(8,128)S(1)} %get-tuple-element.7.part, bf16[4,128,16,128]{3,2,1,0:T(8,128)(2,1)S(1)} %get-tuple-element.8.landed), custom_call_target="tpu_custom_call" | custom-call | tf_op jit(solution)/shard_map/close/pallas_call | solution.py:614

commit v5 on v4

--- a/solution.py
+++ b/solution.py
@@ -373,7 +373,7 @@
     nears = [side * half + lax.rem(inp + d, half) for d in range(half)]
     cores = [lax.rem(tm + d, n_tm) for d in range(n_tm)]
 
-    def dispatch(i, place):
+    def dispatch(i, place, far_first=True):
         send[i] = (stage[...] * (1.0 / GAIN)).reshape(n_dev, 2 * STEP, in_rows).astype(send.dtype)
         group = place // SPAN
         target = landed.at[group, me * SPAN + place % SPAN]
@@ -385,12 +385,10 @@
                 device_id=(inp2, tm2), device_id_type=pl.DeviceIdType.MESH,
             ).start()
 
-        for row in fars:
-            for core in cores:
-                post(row, core)
-        for d, row in enumerate(nears):
-            for core in cores[d == 0 :]:
-                post(row, core)
+        far = [(row, core) for row in fars for core in cores]
+        near = [(row, core) for row in nears for core in cores][1:]
+        for row, core in far + near if far_first else near + far:
+            post(row, core)
         target[...] = send[i, me]
 
     def advance(i, skip=0, stop=STEP + taps - 1):
@@ -429,7 +427,7 @@
             total = head[q, rows, :]
             s = q * STEP + k
             stage[rows, :] = total + tail_in[s] if s < taps - 1 else total
-        dispatch(q, steps - heads + q)
+        dispatch(q, steps - heads + q, False)
 
     history = pltpu.make_async_remote_copy(
         src_ref=tail_out, dst_ref=tail_in, send_sem=tail_send, recv_sem=tail_recv,
@@ -544,8 +542,9 @@
     pack(landed.at[landed.shape[0] - 1], wide, cross, turned)
     scale = 1.0 / spectra
     copies = []
-    for b in range(part.shape[1] // BLOCK):
-        rows = slice(b * BLOCK, (b + 1) * BLOCK)
+    edges = [0, BLOCK // 2, *range(BLOCK, part.shape[1] + 1, BLOCK)]
+    for low, high in zip(edges, edges[1:]):
+        rows = slice(low, high)
         left = turned[rows, :]
         for p, right in enumerate((wide, cross)):
             term = jnp.dot(left, right[...], preferred_element_type=jnp.float32)

time: 62.4 us -> 62.3 us (level)
  no operation moved by 1% of the time
where the time goes in v5:
time: 62.3 us; the launch traced here: 62.2 us
  Pallas kernels  62.2 us (100%)
    pallas_call x1, Pallas kernels, stream_device(): pl.pallas_call(functools.partial(stream_kernel, n_inp, n_tm), out_shape=[...  58.5 us
    pallas_call x1, Pallas kernels, stream_device(): pl.pallas_call(functools.partial(close_kernel, n_tm * steps * STEP), out_...  3.7 us

profile of v5, /device:TPU:0, one launch (start us, length us, event | category | flops | bytes accessed | tf_op | source)
XLA Modules:
  0.0 62.2 jit_solution(389622638348565626)
XLA Ops:
  0.0 58.5 %stream.1 = (f32[2,1024,1024]{2,1,0:T(8,128)S(1)}, bf16[4,128,16,128]{3,2,1,0:T(8,128)(2,1)S(1)}) custom-call(bf16[128,65536]{1,0:T(8,128)(2,1)} %volt.1, f32[16,512]{1,0:T(8,128)} %coef_from.1, f32[64,512]{1,0:T(8,128)} %constant.2.clone.table_from), custom_call_target="tpu_custom_call" | custom-call | tf_op jit(solution)/shard_map/stream/pallas_call | solution.py:582
  58.5 3.7 %close.1 = f32[1,2,1024,1024]{3,2,1,0:T(8,128)} custom-call(f32[2,1024,1024]{2,1,0:T(8,128)S(1)} %get-tuple-element.7.part, bf16[4,128,16,128]{3,2,1,0:T(8,128)(2,1)S(1)} %get-tuple-element.8.landed), custom_call_target="tpu_custom_call" | custom-call | tf_op jit(solution)/shard_map/close/pallas_call | solution.py:613
